TPU v7x, 32 devices: a whole 2x2x4 slice. The times are simulated.
32 devices in a mesh: head: 2 (over y), seq: 16 (over z, x, core).
Axes of the slice: x: 2, y: 2, z: 4, core: 2. Of those that a mesh axis runs over, the one named last changes fastest.
Arguments:
- queries: bfloat16 [2048, 4096], P(('seq', 'head')), may hold values from -20 to 20
- keys: bfloat16 [2048, 1024], P(('seq', 'head')), may hold values from -5 to 5
- values: bfloat16 [2048, 1024], P(('seq', 'head')), may hold values from -6 to 6
Outputs:
- attended: bfloat16 [2048, 4096], P(('seq', 'head'))
All inputs are finite; a program needn't handle non-finite values.
Results may differ from a plain program's by a relative error of at most 0.0041.
Values may be sent and summed in bfloat16 or wider, within the bound.
No kernel may reach another device: no remote copies, remote signals or barrier semaphores. Data moves between devices by JAX's collectives and lax.ppermute only.
A program may use at most 64 MiB of HBM per device.

v0:
```python
import math
import jax
import jax.numpy as jnp
from jax import lax
from jax.sharding import PartitionSpec as P

HEAD_DIM = 128


def update_state(state, query_half, query_pos, key_piece, value_piece, key_pos):
    largest, total, summed = state
    score = jnp.einsum("tkgd,pkd->tkgp", query_half, key_piece, preferred_element_type=jnp.float32)
    score = score / math.sqrt(query_half.shape[-1])
    allowed = (key_pos[None, :] <= query_pos[:, None])[:, None, None, :]
    score = jnp.where(allowed, score, jnp.float32(-1e30))
    new_largest = jnp.maximum(largest, jnp.max(score, axis=-1))
    weight = jnp.where(allowed, jnp.exp(score - new_largest[..., None]), jnp.float32(0.0))
    total = jnp.sum(weight, axis=-1)
    product = jnp.einsum(
        "tkgp,pkd->tkgd",
        weight.astype(jnp.bfloat16),
        value_piece,
        preferred_element_type=jnp.float32,
    )
    summed = product
    return (new_largest, total, summed)


def on_device(queries, keys, values):
    q_local, k_local, v_local = (
        lax.all_to_all(queries, "head", split_axis=1, concat_axis=0, tiled=True),
        lax.all_to_all(keys, "head", split_axis=1, concat_axis=0, tiled=True),
        lax.all_to_all(values, "head", split_axis=1, concat_axis=0, tiled=True),
    )
    tokens = q_local.shape[0]
    half = tokens // 2
    kv_local = k_local.shape[1] // HEAD_DIM
    group = q_local.shape[1] // k_local.shape[1]
    index = lax.axis_index("seq")
    offsets = jnp.arange(half, dtype=jnp.int32)
    later = q_local[half:]
    early_pos = index * tokens + offsets
    later_pos = index * tokens + half + offsets
    query_pos = jnp.stack([early_pos, later_pos])
    halves = jnp.stack([q_local[:half], later]).reshape(2, half, kv_local, group, HEAD_DIM)
    start_state = (
        jnp.full((2, half, kv_local, group), -1e30, jnp.float32),
        jnp.zeros((2, half, kv_local, group), jnp.float32),
        jnp.zeros((2, half, kv_local, group, HEAD_DIM), jnp.float32),
    )
    start = jnp.int32(0)
    key_piece = lax.all_gather(k_local, "seq", axis=0, tiled=True)
    value_piece = lax.all_gather(v_local, "seq", axis=0, tiled=True)
    rows = key_piece.shape[0]
    key_piece = key_piece.reshape(rows, kv_local, HEAD_DIM)
    value_piece = value_piece.reshape(rows, kv_local, HEAD_DIM)
    key_pos = jnp.arange(rows, dtype=jnp.int32)
    results = []
    for which in range(2):
        state = (start_state[0][which], start_state[1][which], start_state[2][which])
        needed = start <= query_pos[which, half - 1]

        def run(current, which=which):
            return update_state(
                current, halves[which], query_pos[which], key_piece, value_piece, key_pos
            )

        def keep(current):
            return current

        results.append(lax.cond(needed, run, keep, state))
    total = jnp.stack([results[0][1], results[1][1]])
    summed = jnp.stack([results[0][2], results[1][2]])
    result = (summed / total[..., None]).reshape(2, half, q_local.shape[1]).astype(jnp.bfloat16)
    later_out = result[1]
    combined = jnp.concatenate([result[0], later_out], axis=0)
    return lax.all_to_all(combined, "head", split_axis=0, concat_axis=1, tiled=True)


def solution(mesh):
    return jax.shard_map(
        on_device,
        mesh=mesh,
        in_specs=(P(("seq", "head"), None), P(("seq", "head"), None), P(("seq", "head"), None)),
        out_specs=P(("seq", "head"), None),
        check_vma=False,
    )
```

profile of v0, /device:TPU:0, one launch (start us, length us, event | category | flops | bytes accessed | tf_op | source)
XLA Modules:
  0.0 142.9 jit_solution(106555980706747682)
XLA Ops:
  6.5 0.9 copy.81
  7.5 8.6 %all_to_all.73 = bf16[64,2,512]{2,0,1:T(8,128)(2,1)} all-to-all(bf16[64,2,512]{2,0,1:T(8,128)(2,1)S(1)} %bitcast.111), channel_id=1, replica_groups=mesh['head'=2,'seq'=16] {'head'}, dimensions={1} | all-to-all | bytes 262144 | tf_op jit(solution)/shard_map/all_to_all | solution.py:32
  16.2 0.9 copy.80
  17.1 7.5 %all_to_all.74 = bf16[64,2,512]{2,0,1:T(8,128)(2,1)} all-to-all(bf16[64,2,512]{2,0,1:T(8,128)(2,1)S(1)} %bitcast.112), channel_id=1, replica_groups=mesh['head'=2,'seq'=16] {'head'}, dimensions={1} | all-to-all | bytes 262144 | tf_op jit(solution)/shard_map/all_to_all | solution.py:33
  24.6 1.9 %copy.79 = bf16[8,2,8,2048]{3,2,0,1:T(8,128)(2,1)} copy(bf16[8,2,8,2048]{3,2,1,0:T(8,128)(2,1)} %bitcast.108) | data formatting | bytes 1048576 | tf_op jit(solution)/shard_map/all_to_all | solution.py:31
  26.5 3.5 %all-to-all-start = ((bf16[64,2,2048]{2,0,1:T(8,128)(2,1)}), bf16[64,2,2048]{2,0,1:T(8,128)(2,1)S(1)}, u32[]{:S(2)}, u32[]{:S(2)}) async-start(bf16[64,2,2048]{2,0,1:T(8,128)(2,1)} %bitcast.98), calls=%async_computation | async-start | bytes 1048576 | tf_op jit(solution)/shard_map/all_to_all | solution.py:31
  32.6 4.0 %all-to-all-done = bf16[64,2,2048]{2,0,1:T(8,128)(2,1)S(1)} async-done(((bf16[64,2,2048]{2,0,1:T(8,128)(2,1)}), bf16[64,2,2048]{2,0,1:T(8,128)(2,1)S(1)}, u32[]{:S(2)}, u32[]{:S(2)}) %all-to-all-start) | async-done | bytes 524320 | tf_op jit(solution)/shard_map/all_to_all | solution.py:31
  37.2 21.2 %all-gather.3.cloned.1.call-done = bf16[2048,512]{1,0:T(8,128)(2,1)} async-done(((bf16[128,512]{1,0:T(8,128)(2,1)}), bf16[2048,512]{1,0:T(8,128)(2,1)}) %all-gather.3.cloned.1.call-update) | async-done | bytes 2097168 | tf_op jit(solution)/shard_map/all_gather | solution.py:52
  58.4 2.9 %copy.49 = bf16[2048,512]{0,1:T(8,128)(2,1)S(1)} copy(bf16[2048,512]{1,0:T(8,128)(2,1)} %all-gather.3.cloned.1.call-done) | data formatting | bytes 4194304 | tf_op jit(solution)/shard_map/all_gather | solution.py:52
  61.3 39.4 %all-gather.5.cloned.1.call-done = bf16[2048,512]{1,0:T(8,128)(2,1)} async-done(((bf16[128,512]{1,0:T(8,128)(2,1)}), bf16[2048,512]{1,0:T(8,128)(2,1)}) %all-gather.5.cloned.1.call-update) | async-done | bytes 2097168 | tf_op jit(solution)/shard_map/all_gather | solution.py:53
  100.7 4.0 %copy.51 = bf16[2048,512]{0,1:T(8,128)(2,1)} copy(bf16[2048,512]{1,0:T(8,128)(2,1)} %all-gather.5.cloned.1.call-done) | data formatting | bytes 4194304 | tf_op jit(solution)/shard_map/all_gather | solution.py:53
  104.7 8.9 %conditional.2 = (f32[1,64,4,4]{1,3,2,0:T(4,128)S(1)}, f32[1,64,2048]{2,1,0:T(8,128)S(1)}) conditional(s32[]{:T(128)} %bitcast.12, () %tuple.29, (s32[2048]{0:T(1024)S(1)}, s32[]{:T(128)}, s32[64]{0:T(128)S(1)}, bf16[2,64,4,4,128]{4,3,2,1,0:T(4,128)(2,1)S(1)}, bf16[2048,4,128]{0,2,1:T(8,128)(2,1)S(1)}, ...), branch_computations={%region_0.0_spmd, %region_1.4_spmd} | conditional | flops 1101134848 | bytes 42238768 | solution.py:71
  105.1 1.7 %fusion = (f32[64,4,4]{0,2,1:T(4,128)S(1)}, f32[4,2048,64,4]{1,2,3,0:T(8,128)S(1)}) fusion(pred[64,2048]{1,0:T(8,128)(4,1)S(1)} %broadcast_compare_fusion, bf16[2,64,4,4,128]{4,1,3,2,0:T(8,128)(2,1)S(1)} %copy.52, bf16[2048,4,128]{0,2,1:T(8,128)(2,1)S(1)} %get-tuple-element.97), kind=kOutput, calls=%fused_computation.2 | convolution fusion | flops 543161344 | bytes 10883072 | tf_op jit(solution)/shard_map/cond/branch_1_fun/tkgd,pkd->tkgp/dot_general | solution.py:12
  106.8 1.9 %fusion.9 = f32[64,4,4,128]{3,0,2,1:T(8,128)S(1)} fusion(bf16[2048,4,128]{0,2,1:T(8,128)(2,1)S(1)} %copy-done, f32[4,2048,64,4]{1,2,3,0:T(8,128)S(1)} %get-tuple-element.106, f32[64,4,4]{0,2,1:T(4,128)S(1)} %broadcast_maximum_fusion, pred[64,2048]{1,0:T(8,128)(4,1)S(1)} %broadcast_compare_fusion), kind=kOutput, calls=%fused_computation.10 | convolution fusion | flops 547356672 | bytes 11145216 | tf_op jit(solution)/shard_map/cond/branch_1_fun/tkgp,pkd->tkgd/dot_general | solution.py:19
  108.7 2.5 %fusion.2 = f32[64,4,4]{0,2,1:T(4,128)S(1)} fusion(f32[4,2048,64,4]{1,2,3,0:T(8,128)S(1)} %get-tuple-element.106, f32[64,4,4]{0,2,1:T(4,128)S(1)} %broadcast_maximum_fusion, pred[64,2048]{1,0:T(8,128)(4,1)S(1)} %broadcast_compare_fusion), kind=kLoop, calls=%fused_computation.4 | loop fusion | flops 10484736 | bytes 8527872 | tf_op jit(solution)/shard_map/cond/branch_1_fun/reduce_sum | solution.py:18
  111.2 1.1 copy.45
  112.4 1.3 stack.31
  113.6 8.0 %conditional.3 = (f32[1,64,4,4]{1,3,2,0:T(4,128)S(1)}, f32[1,64,2048]{2,1,0:T(8,128)}) conditional(s32[]{:T(128)} %bitcast.20, () %tuple.31, (s32[2048]{0:T(1024)S(1)}, s32[]{:T(128)}, s32[64]{0:T(128)S(1)}, bf16[2,64,4,4,128]{4,3,2,1,0:T(4,128)(2,1)S(1)}, bf16[2048,4,128]{0,2,1:T(8,128)(2,1)S(1)}, /*index=5*/bf16[2048,4,128]{0,2,1:T(8,128)(2,1)}) %tuple.56), branch_computations={%region_4.5_spmd, %region_5.8_spmd} | conditional | flops 1101134848 | bytes 42238768 | solution.py:71
  114.1 1.7 %fusion.17 = (f32[64,4,4]{0,2,1:T(4,128)S(1)}, f32[4,2048,64,4]{1,2,3,0:T(8,128)S(1)}) fusion(pred[64,2048]{1,0:T(8,128)(4,1)S(1)} %broadcast_compare_fusion.1, bf16[2,64,4,4,128]{4,1,3,2,0:T(8,128)(2,1)S(1)} %copy.55, bf16[2048,4,128]{0,2,1:T(8,128)(2,1)S(1)} %get-tuple-element.103), kind=kOutput, calls=%fused_computation.20 | convolution fusion | flops 543161344 | bytes 10883072 | tf_op jit(solution)/shard_map/cond/branch_1_fun/tkgd,pkd->tkgp/dot_general | solution.py:12
  115.8 1.9 %fusion.26 = f32[64,4,4,128]{3,0,2,1:T(8,128)S(1)} fusion(bf16[2048,4,128]{0,2,1:T(8,128)(2,1)S(1)} %copy-done.1, f32[4,2048,64,4]{1,2,3,0:T(8,128)S(1)} %get-tuple-element.108, f32[64,4,4]{0,2,1:T(4,128)S(1)} %broadcast_maximum_fusion.1, pred[64,2048]{1,0:T(8,128)(4,1)S(1)} %broadcast_compare_fusion.1), kind=kOutput, calls=%fused_computation.28 | convolution fusion | flops 547356672 | bytes 11145216 | tf_op jit(solution)/shard_map/cond/branch_1_fun/tkgp,pkd->tkgd/dot_general | solution.py:19
  117.8 2.5 %fusion.19 = f32[64,4,4]{0,2,1:T(4,128)S(1)} fusion(f32[4,2048,64,4]{1,2,3,0:T(8,128)S(1)} %get-tuple-element.108, f32[64,4,4]{0,2,1:T(4,128)S(1)} %broadcast_maximum_fusion.1, pred[64,2048]{1,0:T(8,128)(4,1)S(1)} %broadcast_compare_fusion.1), kind=kLoop, calls=%fused_computation.22 | loop fusion | flops 10484736 | bytes 8527872 | tf_op jit(solution)/shard_map/cond/branch_1_fun/reduce_sum | solution.py:18
  120.7 1.0 stack.35
  122.9 1.2 fusion.34
  124.2 11.1 %all_to_all.75 = bf16[2,64,2048]{2,1,0:T(8,128)(2,1)S(1)} all-to-all(bf16[2,64,2048]{2,1,0:T(8,128)(2,1)S(1)} %bitcast.106), channel_id=1, replica_groups=mesh['head'=2,'seq'=16] {'head'}, dimensions={0} | all-to-all | bytes 1048576 | tf_op jit(solution)/shard_map/all_to_all | solution.py:77
  (37 shorter events, 5.0 us)
Async XLA Ops:
  6.5 51.8 %all-gather.3.cloned.1.call-start = ((), (), s32[]{:S(2)}) async-start(), calls=%async_computation.4 | async-start | bytes 2228224 | tf_op jit(solution)/shard_map/all_gather | solution.py:52
  16.1 84.6 %all-gather.5.cloned.1.call-start = ((), (), s32[]{:S(2)}) async-start(), calls=%async_computation.5 | async-start | bytes 2228224 | tf_op jit(solution)/shard_map/all_gather | solution.py:53
  26.5 10.1 %all-to-all-start = ((bf16[64,2,2048]{2,0,1:T(8,128)(2,1)}), bf16[64,2,2048]{2,0,1:T(8,128)(2,1)S(1)}, u32[]{:S(2)}, u32[]{:S(2)}) async-start(bf16[64,2,2048]{2,0,1:T(8,128)(2,1)} %bitcast.98), calls=%async_computation | async-start | bytes 1048576 | tf_op jit(solution)/shard_map/all_to_all | solution.py:31
  105.0 1.7 %copy-start = (bf16[2048,4,128]{0,2,1:T(8,128)(2,1)S(1)}, bf16[2048,4,128]{0,2,1:T(8,128)(2,1)}, u32[]{:S(2)}) copy-start(bf16[2048,4,128]{0,2,1:T(8,128)(2,1)} %get-tuple-element.98) | copy-start | bytes 6291460 | tf_op jit(solution)/shard_map/cond
  114.1 1.7 %copy-start.1 = (bf16[2048,4,128]{0,2,1:T(8,128)(2,1)S(1)}, bf16[2048,4,128]{0,2,1:T(8,128)(2,1)}, u32[]{:S(2)}) copy-start(bf16[2048,4,128]{0,2,1:T(8,128)(2,1)} %get-tuple-element.104) | copy-start | bytes 6291460 | tf_op jit(solution)/shard_map/cond
Sparse Core Ops, SparseCore 0:
  16.2 42.0 all-gather.2
  60.5 40.1 all-gather.4
where the time goes:
time: 144 us; the launch traced here: 143 us
  waiting for transfers between devices  64.6 us (45%)
  blocking collectives  27.2 us (19%)
  local copies, waits for them, and re-layouts  18.5 us (13%)
  between operations  14.8 us (10%)
  matrix products  7.21 us (5%)
  other arithmetic  6.63 us (5%)
  starting transfers between devices  3.53 us (2%)
    all_gather x1, waiting for transfers between devices, on_device(): value_piece = lax.all_gather(v_local, 'seq', axis=0, tiled=True)  39.4 us
    all_gather x1, waiting for transfers between devices, on_device(): key_piece = lax.all_gather(k_local, 'seq', axis=0, tiled=True)  21.2 us
    all_to_all x1, blocking collectives, on_device(): lax.all_to_all(combined, 'head', split_axis=0, concat_axis=1, tiled=True)  11.1 us
    all_to_all x1, blocking collectives, on_device(): lax.all_to_all(keys, 'head', split_axis=1, concat_axis=0, tiled=True)  8.64 us
    all_to_all x1, blocking collectives, on_device(): lax.all_to_all(values, 'head', split_axis=1, concat_axis=0, tiled=True)  7.52 us
    reduce_sum x2, other arithmetic, update_state(): total = jnp.sum(weight, axis=-1)  5.08 us
    all_to_all x1, waiting for transfers between devices, on_device(): lax.all_to_all(queries, 'head', split_axis=1, concat_axis=0, tiled=True)  3.99 us
    all_gather x1, local copies, waits for them, and re-layouts, on_device(): value_piece = lax.all_gather(v_local, 'seq', axis=0, tiled=True)  3.95 us
  transfers between devices with their start and end apart: 3, of which 3 were waited for; matrix products, arithmetic and copies ran while one was open for 5% of the time, Pallas kernels for 0%

commit v1 on v0

--- a/solution.py
+++ b/solution.py
@@ -29,7 +29,10 @@
 def on_device(queries, keys, values):
     q_local, k_local, v_local = (
         lax.all_to_all(queries, "head", split_axis=1, concat_axis=0, tiled=True),
-        lax.all_to_all(keys, "head", split_axis=1, concat_axis=0, tiled=True),
+        jnp.concatenate(
+            lax.all_to_all(jnp.stack(jnp.split(keys, lax.axis_size("head"), axis=1)), "head", 0, 0),
+            axis=0,
+        ),
         lax.all_to_all(values, "head", split_axis=1, concat_axis=0, tiled=True),
     )
     tokens = q_local.shape[0]

time: 144 us -> 143 us (level)
    all_gather x1, waiting for transfers between devices: 39.4 us -> 21.2 us  [on_device(): value_piece = lax.all_gather(v_local, 'seq', axis=0, tiled=True)]
    all_gather x1, waiting for transfers between devices: 21.2 us -> 38.4 us  [on_device(): key_piece = lax.all_gather(k_local, 'seq', axis=0, tiled=True)]
  transfers between devices with their start and end apart: 3 -> 3, of which waited for: 3 -> 3; matrix products, arithmetic and copies ran while one was open for 5% -> 6% of each run, Pallas kernels for 0% -> 0%
where the time goes in v1:
time: 143 us; the launch traced here: 142 us
  waiting for transfers between devices  63.8 us (45%)
  blocking collectives  27.2 us (19%)
  local copies, waits for them, and re-layouts  18.4 us (13%)
  between operations  14.7 us (10%)
  matrix products  7.21 us (5%)
  other arithmetic  6.65 us (5%)
  starting transfers between devices  3.53 us (2%)
    all_gather x1, waiting for transfers between devices, on_device(): key_piece = lax.all_gather(k_local, 'seq', axis=0, tiled=True)  38.4 us
    all_gather x1, waiting for transfers between devices, on_device(): value_piece = lax.all_gather(v_local, 'seq', axis=0, tiled=True)  21.2 us
    all_to_all x1, blocking collectives, on_device(): lax.all_to_all(combined, 'head', split_axis=0, concat_axis=1, tiled=True)  11.1 us
    all_to_all x1, blocking collectives, on_device(): lax.all_to_all(values, 'head', split_axis=1, concat_axis=0, tiled=True)  8.64 us
    all_to_all x1, blocking collectives, on_device(): lax.all_to_all(jnp.stack(jnp.split(keys, lax.axis_size('head'), axis=1)),...  7.52 us
    reduce_sum x2, other arithmetic, update_state(): total = jnp.sum(weight, axis=-1)  5.08 us
    all_to_all x1, waiting for transfers between devices, on_device(): lax.all_to_all(queries, 'head', split_axis=1, concat_axis=0, tiled=True)  4.2 us
    all_gather x1, local copies, waits for them, and re-layouts, on_device(): value_piece = lax.all_gather(v_local, 'seq', axis=0, tiled=True)  3.94 us
  transfers between devices with their start and end apart: 3, of which 3 were waited for; matrix products, arithmetic and copies ran while one was open for 6% of the time, Pallas kernels for 0%

profile of v1, /device:TPU:0, one launch (start us, length us, event | category | flops | bytes accessed | tf_op | source)
XLA Modules:
  0.0 141.9 jit_solution(1181739595264005741)
XLA Ops:
  6.5 0.9 copy.75
  7.5 8.6 %all_to_all.59 = bf16[64,2,512]{2,0,1:T(8,128)(2,1)} all-to-all(bf16[64,2,512]{2,0,1:T(8,128)(2,1)S(1)} %bitcast.109), channel_id=1, replica_groups=mesh['head'=2,'seq'=16] {'head'}, dimensions={1} | all-to-all | bytes 262144 | tf_op jit(solution)/shard_map/all_to_all | solution.py:36
  16.2 0.9 slice_bitcast_fusion.7
  17.1 7.5 %all_to_all.60 = bf16[2,64,512]{2,1,0:T(8,128)(2,1)} all-to-all(bf16[2,64,512]{2,1,0:T(8,128)(2,1)S(1)} %pad_maximum_fusion.1), channel_id=1, replica_groups=mesh['head'=2,'seq'=16] {'head'}, dimensions={0} | all-to-all | bytes 262144 | tf_op jit(solution)/shard_map/all_to_all | solution.py:33
  24.6 1.9 %copy.74 = bf16[8,2,8,2048]{3,2,0,1:T(8,128)(2,1)} copy(bf16[8,2,8,2048]{3,2,1,0:T(8,128)(2,1)} %bitcast.106) | data formatting | bytes 1048576 | tf_op jit(solution)/shard_map/all_to_all | solution.py:31
  26.5 3.5 %all-to-all-start = ((bf16[64,2,2048]{2,0,1:T(8,128)(2,1)}), bf16[64,2,2048]{2,0,1:T(8,128)(2,1)S(1)}, u32[]{:S(2)}, u32[]{:S(2)}) async-start(bf16[64,2,2048]{2,0,1:T(8,128)(2,1)} %bitcast.97), calls=%async_computation | async-start | bytes 1048576 | tf_op jit(solution)/shard_map/all_to_all | solution.py:31
  32.4 4.2 %all-to-all-done = bf16[64,2,2048]{2,0,1:T(8,128)(2,1)S(1)} async-done(((bf16[64,2,2048]{2,0,1:T(8,128)(2,1)}), bf16[64,2,2048]{2,0,1:T(8,128)(2,1)S(1)}, u32[]{:S(2)}, u32[]{:S(2)}) %all-to-all-start) | async-done | bytes 524320 | tf_op jit(solution)/shard_map/all_to_all | solution.py:31
  37.2 21.2 %all-gather.5.cloned.1.call-done = bf16[2048,512]{1,0:T(8,128)(2,1)} async-done(((bf16[128,512]{1,0:T(8,128)(2,1)}), bf16[2048,512]{1,0:T(8,128)(2,1)}) %all-gather.5.cloned.1.call-update) | async-done | bytes 2097168 | tf_op jit(solution)/shard_map/all_gather | solution.py:56
  58.4 3.9 %copy.48 = bf16[2048,512]{0,1:T(8,128)(2,1)} copy(bf16[2048,512]{1,0:T(8,128)(2,1)} %all-gather.5.cloned.1.call-done) | data formatting | bytes 4194304 | tf_op jit(solution)/shard_map/all_gather | solution.py:56
  62.3 38.4 %all-gather.3.cloned.1.call-done = bf16[2048,512]{1,0:T(8,128)(2,1)} async-done(((bf16[128,512]{1,0:T(8,128)(2,1)}), bf16[2048,512]{1,0:T(8,128)(2,1)}) %all-gather.3.cloned.1.call-update) | async-done | bytes 2097168 | tf_op jit(solution)/shard_map/all_gather | solution.py:55
  100.7 2.9 %copy.46 = bf16[2048,512]{0,1:T(8,128)(2,1)S(1)} copy(bf16[2048,512]{1,0:T(8,128)(2,1)} %all-gather.3.cloned.1.call-done) | data formatting | bytes 4194304 | tf_op jit(solution)/shard_map/all_gather | solution.py:55
  103.7 8.9 %conditional.2 = (f32[1,64,4,4]{1,3,2,0:T(4,128)S(1)}, f32[1,64,2048]{2,1,0:T(8,128)S(1)}) conditional(s32[]{:T(128)} %bitcast.12, () %tuple.29, (s32[2048]{0:T(1024)S(1)}, s32[]{:T(128)}, s32[64]{0:T(128)S(1)}, bf16[2,64,4,4,128]{4,3,2,1,0:T(4,128)(2,1)S(1)}, bf16[2048,4,128]{0,2,1:T(8,128)(2,1)S(1)}, ...), branch_computations={%region_0.0_spmd, %region_1.4_spmd} | conditional | flops 1101134848 | bytes 42238768 | solution.py:74
  104.0 1.7 %fusion = (f32[64,4,4]{0,2,1:T(4,128)S(1)}, f32[4,2048,64,4]{1,2,3,0:T(8,128)S(1)}) fusion(pred[64,2048]{1,0:T(8,128)(4,1)S(1)} %broadcast_compare_fusion, bf16[2,64,4,4,128]{4,1,3,2,0:T(8,128)(2,1)S(1)} %copy.49, bf16[2048,4,128]{0,2,1:T(8,128)(2,1)S(1)} %get-tuple-element.97), kind=kOutput, calls=%fused_computation.2 | convolution fusion | flops 543161344 | bytes 10883072 | tf_op jit(solution)/shard_map/cond/branch_1_fun/tkgd,pkd->tkgp/dot_general | solution.py:12
  105.8 1.9 %fusion.9 = f32[64,4,4,128]{3,0,2,1:T(8,128)S(1)} fusion(bf16[2048,4,128]{0,2,1:T(8,128)(2,1)S(1)} %copy-done, f32[4,2048,64,4]{1,2,3,0:T(8,128)S(1)} %get-tuple-element.106, f32[64,4,4]{0,2,1:T(4,128)S(1)} %broadcast_maximum_fusion, pred[64,2048]{1,0:T(8,128)(4,1)S(1)} %broadcast_compare_fusion), kind=kOutput, calls=%fused_computation.10 | convolution fusion | flops 547356672 | bytes 11145216 | tf_op jit(solution)/shard_map/cond/branch_1_fun/tkgp,pkd->tkgd/dot_general | solution.py:19
  107.7 2.5 %fusion.2 = f32[64,4,4]{0,2,1:T(4,128)S(1)} fusion(f32[4,2048,64,4]{1,2,3,0:T(8,128)S(1)} %get-tuple-element.106, f32[64,4,4]{0,2,1:T(4,128)S(1)} %broadcast_maximum_fusion, pred[64,2048]{1,0:T(8,128)(4,1)S(1)} %broadcast_compare_fusion), kind=kLoop, calls=%fused_computation.4 | loop fusion | flops 10484736 | bytes 8527872 | tf_op jit(solution)/shard_map/cond/branch_1_fun/reduce_sum | solution.py:18
  110.2 1.1 copy.43
  111.4 1.3 stack.37
  112.6 8.0 %conditional.3 = (f32[1,64,4,4]{1,3,2,0:T(4,128)S(1)}, f32[1,64,2048]{2,1,0:T(8,128)}) conditional(s32[]{:T(128)} %bitcast.21, () %tuple.31, (s32[2048]{0:T(1024)S(1)}, s32[]{:T(128)}, s32[64]{0:T(128)S(1)}, bf16[2,64,4,4,128]{4,3,2,1,0:T(4,128)(2,1)S(1)}, bf16[2048,4,128]{0,2,1:T(8,128)(2,1)S(1)}, /*index=5*/bf16[2048,4,128]{0,2,1:T(8,128)(2,1)}) %tuple.57), branch_computations={%region_4.5_spmd, %region_5.8_spmd} | conditional | flops 1101134848 | bytes 42238768 | solution.py:74
  113.1 1.7 %fusion.17 = (f32[64,4,4]{0,2,1:T(4,128)S(1)}, f32[4,2048,64,4]{1,2,3,0:T(8,128)S(1)}) fusion(pred[64,2048]{1,0:T(8,128)(4,1)S(1)} %broadcast_compare_fusion.1, bf16[2,64,4,4,128]{4,1,3,2,0:T(8,128)(2,1)S(1)} %copy.52, bf16[2048,4,128]{0,2,1:T(8,128)(2,1)S(1)} %get-tuple-element.103), kind=kOutput, calls=%fused_computation.20 | convolution fusion | flops 543161344 | bytes 10883072 | tf_op jit(solution)/shard_map/cond/branch_1_fun/tkgd,pkd->tkgp/dot_general | solution.py:12
  114.8 1.9 %fusion.26 = f32[64,4,4,128]{3,0,2,1:T(8,128)S(1)} fusion(bf16[2048,4,128]{0,2,1:T(8,128)(2,1)S(1)} %copy-done.1, f32[4,2048,64,4]{1,2,3,0:T(8,128)S(1)} %get-tuple-element.108, f32[64,4,4]{0,2,1:T(4,128)S(1)} %broadcast_maximum_fusion.1, pred[64,2048]{1,0:T(8,128)(4,1)S(1)} %broadcast_compare_fusion.1), kind=kOutput, calls=%fused_computation.28 | convolution fusion | flops 547356672 | bytes 11145216 | tf_op jit(solution)/shard_map/cond/branch_1_fun/tkgp,pkd->tkgd/dot_general | solution.py:19
  116.8 2.5 %fusion.19 = f32[64,4,4]{0,2,1:T(4,128)S(1)} fusion(f32[4,2048,64,4]{1,2,3,0:T(8,128)S(1)} %get-tuple-element.108, f32[64,4,4]{0,2,1:T(4,128)S(1)} %broadcast_maximum_fusion.1, pred[64,2048]{1,0:T(8,128)(4,1)S(1)} %broadcast_compare_fusion.1), kind=kLoop, calls=%fused_computation.22 | loop fusion | flops 10484736 | bytes 8527872 | tf_op jit(solution)/shard_map/cond/branch_1_fun/reduce_sum | solution.py:18
  119.7 1.0 stack.41
  121.9 1.2 fusion.34
  123.2 11.1 %all_to_all.61 = bf16[2,64,2048]{2,1,0:T(8,128)(2,1)S(1)} all-to-all(bf16[2,64,2048]{2,1,0:T(8,128)(2,1)S(1)} %bitcast.104), channel_id=1, replica_groups=mesh['head'=2,'seq'=16] {'head'}, dimensions={0} | all-to-all | bytes 1048576 | tf_op jit(solution)/shard_map/all_to_all | solution.py:80
  (38 shorter events, 4.9 us)
Async XLA Ops:
  6.5 51.8 %all-gather.5.cloned.1.call-start = ((), (), s32[]{:S(2)}) async-start(), calls=%async_computation.5 | async-start | bytes 2228224 | tf_op jit(solution)/shard_map/all_gather | solution.py:56
  16.1 84.6 %all-gather.3.cloned.1.call-start = ((), (), s32[]{:S(2)}) async-start(), calls=%async_computation.4 | async-start | bytes 2228224 | tf_op jit(solution)/shard_map/all_gather | solution.py:55
  26.5 10.1 %all-to-all-start = ((bf16[64,2,2048]{2,0,1:T(8,128)(2,1)}), bf16[64,2,2048]{2,0,1:T(8,128)(2,1)S(1)}, u32[]{:S(2)}, u32[]{:S(2)}) async-start(bf16[64,2,2048]{2,0,1:T(8,128)(2,1)} %bitcast.97), calls=%async_computation | async-start | bytes 1048576 | tf_op jit(solution)/shard_map/all_to_all | solution.py:31
  104.0 1.7 %copy-start = (bf16[2048,4,128]{0,2,1:T(8,128)(2,1)S(1)}, bf16[2048,4,128]{0,2,1:T(8,128)(2,1)}, u32[]{:S(2)}) copy-start(bf16[2048,4,128]{0,2,1:T(8,128)(2,1)} %get-tuple-element.98) | copy-start | bytes 6291460 | tf_op jit(solution)/shard_map/cond
  113.1 1.7 %copy-start.1 = (bf16[2048,4,128]{0,2,1:T(8,128)(2,1)S(1)}, bf16[2048,4,128]{0,2,1:T(8,128)(2,1)}, u32[]{:S(2)}) copy-start(bf16[2048,4,128]{0,2,1:T(8,128)(2,1)} %get-tuple-element.104) | copy-start | bytes 6291460 | tf_op jit(solution)/shard_map/cond
Sparse Core Ops, SparseCore 0:
  16.2 42.0 all-gather.4
  60.5 40.1 all-gather.2
